TPU v7x, 32 devices: a whole 2x2x4 slice. The times are simulated.
32 devices in a mesh: group: 4 (over z), tensor: 8 (over y, x, core).
Axes of the slice: x: 2, y: 2, z: 4, core: 2. Of those that a mesh axis runs over, the one named last changes fastest.
Arguments:
- key_value_cache: bfloat16 [256, 1024, 256], P(('group', 'tensor')), may hold values from -8 to 8
- queries: bfloat16 [32, 48, 128], P('group'), may hold values from -200 to 200
- fresh_key_value: bfloat16 [32, 8, 256], P('group'), may hold values from -6 to 6
- lengths: int32 [32], P('group'), may hold values from 2 to 1023
- residual: bfloat16 [32, 6144], P('group'), may hold values from -100 to 100
- norm_gain: float32 [6144], replicated, may hold values from 0.1 to 1.9
- router_weight: bfloat16 [6144, 8], replicated, may hold values from -0.078125 to 0.078125
- routing: int32 [32, 2], P('group'), may hold values from 0 to 7, all different within a row
- expert_gate: bfloat16 [8, 6144, 8192], P(None, 'group', 'tensor'), may hold values from -0.078125 to 0.078125
- expert_up: bfloat16 [8, 6144, 8192], P(None, 'group', 'tensor'), may hold values from -0.078125 to 0.078125
Outputs:
- updated: bfloat16 [32, 6144], P('group')
- expert_hidden: bfloat16 [32, 2, 8192], P('group', None, 'tensor')
- new_cache: bfloat16 [32, 8, 1024, 256], P('group', None, 'tensor')
Inputs may be any that keep to these rules, and one draw needn't show every extreme that they name: Slot lengths[s] of sequence s receives its new token. `routing`: A token's two experts differ.
All inputs are finite; a program needn't handle non-finite values.
Results may differ from a plain program's by a relative error of at most 0.028.
Values may be sent and summed in bfloat16 or wider, within the bound.
A program may use at most 128 MiB of HBM per device.

v0:
```python
import functools
import math

import jax
import jax.numpy as jnp
from jax import lax
from jax.experimental import pallas as pl
from jax.experimental.pallas import tpu as pltpu
from jax.sharding import PartitionSpec as P

MESH = pl.DeviceIdType.MESH
LANES = 128
NT = (((1,), (1,)), ((), ()))


def flip(rank, bits, count):
    out, step = rank, 1
    while step < count:
        if bits & step:
            out = out + step * (1 - 2 * (rank // step % 2))
        step *= 2
    return out


def swapped(bits, count):
    if count < 8 or (bits >> 1) % 2 == (bits >> 2) % 2:
        return bits
    return bits ^ 6


def kernel(
    n_t,
    n_g,
    cache_hbm,
    queries_ref,
    fresh_ref,
    lengths_ref,
    residual_ref,
    gain_ref,
    router_ref,
    routing_ref,
    gate_hbm,
    up_hbm,
    updated_ref,
    hidden_ref,
    out_cache,
    cache_v,
    gate_v,
    up_v,
    heads_b,
    heads_v,
    normed_v,
    x_send,
    x_recv,
    picked,
    p_send,
    p_recv,
    load_sem,
    gate_sem,
    up_sem,
    own_sem,
    a_send_sem,
    a_recv_sem,
    b_send_sem,
    b_recv_sem,
    h_send_sem,
    h_recv_sem,
    x_send_sem,
    x_recv_sem,
    p_send_sem,
    p_recv_sem,
):
    tensor = lax.axis_index("tensor")
    group = lax.axis_index("group")
    pairs, slots, width = cache_v.shape
    head = width // 2
    span = slots // n_t
    first = max(1, pairs // 2)
    seqs, q_heads, _ = queries_ref.shape
    kv_heads = fresh_ref.shape[1]
    per = q_heads // kv_heads
    experts = gate_v.shape[0]
    depth = gate_v.shape[1]
    columns = residual_ref.shape[1]
    shares = heads_v.shape[1]

    load = pltpu.make_async_copy(cache_hbm, cache_v, load_sem)
    load.start()
    for e in range(experts):
        pltpu.make_async_copy(gate_hbm.at[e], gate_v.at[e], gate_sem.at[e]).start()
        pltpu.make_async_copy(up_hbm.at[e], up_v.at[e], up_sem.at[e]).start()

    odd = tensor % 2
    t_peers = [
        (1 - odd) * flip(tensor, d, n_t) + odd * flip(tensor, swapped(d, n_t), n_t)
        for d in range(1, n_t)
    ]
    g_peers = [flip(group, d, n_g) for d in range(1, n_g)]
    barrier = pltpu.get_barrier_semaphore()
    for peer in t_peers:
        pl.semaphore_signal(barrier, inc=1, device_id={"tensor": peer}, device_id_type=MESH)
    for peer in g_peers:
        pl.semaphore_signal(barrier, inc=1, device_id={"group": peer}, device_id_type=MESH)
    pl.semaphore_wait(barrier, n_t + n_g - 2)
    load.wait()

    def block(begin, count, d, send, recv):
        peer = t_peers[d - 1]
        return pltpu.make_async_remote_copy(
            src_ref=cache_v.at[pl.ds(begin, count), pl.ds(peer * span, span), :],
            dst_ref=out_cache.at[pl.ds(tensor * pairs + begin, count)],
            send_sem=send.at[d],
            recv_sem=recv.at[d],
            device_id={"tensor": peer},
            device_id_type=MESH,
        )

    hops = {d: bin(d // 2).count("1") for d in range(1, n_t)}
    order = sorted(range(1, n_t), key=lambda d: (hops[d], d % 2, d))
    near = [d for d in order if hops[d] == 1]
    early = [block(0, first, d, a_send_sem, a_recv_sem) for d in near]
    for copy in early:
        copy.start()

    begin = tensor * pairs
    seq = begin // kv_heads
    head0 = begin % kv_heads
    share = tensor % shares
    scale = 1.0 / math.sqrt(head)
    q = queries_ref[seq]
    fresh = fresh_ref[seq]
    length = lengths_ref[seq]
    row = lax.broadcasted_iota(jnp.int32, (q_heads, 1), 0)
    mine = [
        (row >= (head0 + p) * per) & (row < (head0 + p + 1) * per) for p in range(pairs)
    ]
    scores = jnp.zeros((q_heads, slots), jnp.float32)
    for p in range(pairs):
        s = lax.dot_general(q, cache_v[p, :, :head], NT, preferred_element_type=jnp.float32)
        scores = jnp.where(mine[p], s, scores)
    scores = scores * scale
    own_all = lax.dot_general(q, fresh[:, :head], NT, preferred_element_type=jnp.float32) * scale
    wide_row = lax.broadcasted_iota(jnp.int32, (q_heads, kv_heads), 0)
    wide_col = lax.broadcasted_iota(jnp.int32, (q_heads, kv_heads), 1)
    own_mask = (wide_row >= wide_col * per) & (wide_row < (wide_col + 1) * per)
    own_score = jnp.sum(jnp.where(own_mask, own_all, 0.0), axis=1, keepdims=True)
    visible = lax.broadcasted_iota(jnp.int32, (q_heads, slots), 1) < length
    scores = jnp.where(visible, scores, -1e30)
    peak = jnp.maximum(jnp.max(scores, axis=1, keepdims=True), own_score)
    weights = jnp.where(visible, jnp.exp(scores - peak), 0.0)
    own_weight = jnp.exp(own_score - peak)
    denominator = jnp.sum(weights, axis=1, keepdims=True) + own_weight
    rounded = weights.astype(jnp.bfloat16)
    own_rounded = jnp.where(own_mask, own_weight, 0.0).astype(jnp.bfloat16)
    own_value = jnp.dot(own_rounded, fresh[:, head:], preferred_element_type=jnp.float32)
    result = jnp.zeros((q_heads, head), jnp.float32)
    for p in range(pairs):
        o = jnp.dot(rounded, cache_v[p, :, head:], preferred_element_type=jnp.float32)
        result = jnp.where(mine[p], (o + own_value) / denominator, result)
    heads_b[seq, share] = result.astype(jnp.bfloat16)

    h_copies = []
    for d in order:
        copy = pltpu.make_async_remote_copy(
            src_ref=heads_b.at[seq, share],
            dst_ref=heads_b.at[seq, share],
            send_sem=h_send_sem.at[d],
            recv_sem=h_recv_sem.at[d],
            device_id={"tensor": t_peers[d - 1]},
            device_id_type=MESH,
        )
        copy.start()
        h_copies.append(copy)
    late = []
    if first < pairs:
        late = [block(first, pairs - first, d, b_send_sem, b_recv_sem) for d in near]
    late += [block(0, pairs, d, a_send_sem, a_recv_sem) for d in order if hops[d] != 1]
    for copy in late:
        copy.start()
    own = pltpu.make_async_copy(
        cache_v.at[:, pl.ds(tensor * span, span), :],
        out_cache.at[pl.ds(tensor * pairs, pairs)],
        own_sem,
    )
    own.start()
    picked[...] = jnp.zeros_like(picked)
    lane = lax.broadcasted_iota(jnp.int32, (seqs, LANES), 1)
    diagonal = lax.broadcasted_iota(jnp.int32, (seqs, seqs), 0) == lax.broadcasted_iota(
        jnp.int32, (seqs, seqs), 1
    )
    ids = [
        jnp.sum(
            jnp.where(diagonal, routing_ref[k : k + 1, :].astype(jnp.float32), 0.0),
            axis=1,
            keepdims=True,
        )
        for k in range(2)
    ]
    tags = jnp.where(lane == 0, ids[0], jnp.where(lane == 1, ids[1], 0.0)).astype(jnp.bfloat16)
    for g in range(n_g):
        x_send[g, :, depth:] = tags
    for copy in h_copies:
        copy.wait_recv()

    heads_v[...] = heads_b[...].astype(jnp.float32)

    squares = jnp.zeros((seqs, LANES), jnp.float32)
    for c in range(0, columns, LANES):
        add = heads_v[:, 0, c // LANES, :]
        for other in range(1, shares):
            add = add + heads_v[:, other, c // LANES, :]
        u = (residual_ref[:, c : c + LANES].astype(jnp.float32) + add).astype(jnp.bfloat16)
        updated_ref[:, c : c + LANES] = u
        u = u.astype(jnp.float32)
        squares = squares + u * u
    factor = lax.rsqrt(jnp.sum(squares, axis=1, keepdims=True) / columns + 1e-05)
    for c in range(0, columns, LANES):
        u = updated_ref[:, c : c + LANES].astype(jnp.float32)
        n = (u * factor * gain_ref[:, c : c + LANES]).astype(jnp.bfloat16)
        normed_v[:, c : c + LANES] = n
        x_send[c // depth, :, c % depth : c % depth + LANES] = n
    x_copies = []
    for d in range(1, n_g):
        copy = pltpu.make_async_remote_copy(
            src_ref=x_send.at[g_peers[d - 1]],
            dst_ref=x_recv.at[group],
            send_sem=x_send_sem.at[d],
            recv_sem=x_recv_sem.at[d],
            device_id={"group": g_peers[d - 1]},
            device_id_type=MESH,
        )
        copy.start()
        x_copies.append(copy)
    x_recv[group] = x_send[group]
    logits = lax.dot_general(
        normed_v[...], router_ref[...], NT, preferred_element_type=jnp.float32
    )
    expert_col = lax.broadcasted_iota(jnp.int32, (seqs, experts), 1)
    chosen = [
        jnp.sum(jnp.where(expert_col == ids[k].astype(jnp.int32), logits, 0.0), axis=1, keepdims=True)
        for k in range(2)
    ]
    gap = chosen[0] - chosen[1]
    gates = [jax.nn.sigmoid(gap), jax.nn.sigmoid(-gap)]
    for copy in x_copies:
        copy.wait_recv()

    parts = [x_recv[g].astype(jnp.float32) for g in range(n_g)]
    tokens = jnp.concatenate(parts, axis=0)
    x = tokens[:, :depth].astype(jnp.bfloat16)
    tag = tokens[:, depth:]

    def expert(e, carry):
        picks = [tag[:, k : k + 1] == e.astype(jnp.float32) for k in range(2)]
        for which, (hbm, buf, sem) in enumerate(
            ((gate_hbm, gate_v, gate_sem), (up_hbm, up_v, up_sem))
        ):
            pltpu.make_async_copy(hbm.at[e], buf.at[e], sem.at[e]).wait()
            part = jnp.dot(x, buf[e], preferred_element_type=jnp.float32)
            for k in range(2):
                picked[k, which] = jnp.where(picks[k], part, picked[k, which])
        return carry

    lax.fori_loop(0, experts, expert, 0)

    for g in range(n_g):
        p_send[g] = picked[:, :, g * seqs : (g + 1) * seqs, :].astype(jnp.bfloat16)
    p_copies = []
    for d in range(1, n_g):
        copy = pltpu.make_async_remote_copy(
            src_ref=p_send.at[g_peers[d - 1]],
            dst_ref=p_recv.at[group],
            send_sem=p_send_sem.at[d],
            recv_sem=p_recv_sem.at[d],
            device_id={"group": g_peers[d - 1]},
            device_id_type=MESH,
        )
        copy.start()
        p_copies.append(copy)
    p_recv[group] = p_send[group]
    for copy in p_copies:
        copy.wait_recv()
    for k in range(2):
        sums = []
        for which in range(2):
            total = p_recv[0, k, which].astype(jnp.float32)
            for g in range(1, n_g):
                total = total + p_recv[g, k, which].astype(jnp.float32)
            sums.append(total)
        value = gates[k] * (sums[0] / (1.0 + jnp.exp(-sums[0]))) * sums[1]
        hidden_ref[k] = value.astype(jnp.bfloat16)

    for copy in h_copies + x_copies + p_copies:
        copy.wait_send()
    for copy in early + late:
        copy.wait()
    own.wait()


def body(
    n_t,
    n_g,
    key_value_cache,
    queries,
    fresh_key_value,
    lengths,
    residual,
    norm_gain,
    router_weight,
    routing,
    expert_gate,
    expert_up,
):
    pairs, slots, width = key_value_cache.shape
    seqs, q_heads, head = queries.shape
    kv_heads = fresh_key_value.shape[1]
    columns = residual.shape[1]
    experts, depth, units = expert_gate.shape
    span = slots // n_t
    shares = kv_heads // pairs
    any_space = pl.BlockSpec(memory_space=pl.ANY)
    vmem = pl.BlockSpec(memory_space=pltpu.VMEM)
    smem = pl.BlockSpec(memory_space=pltpu.SMEM)
    dma = pltpu.SemaphoreType.DMA
    bf16, f32 = jnp.bfloat16, jnp.float32
    updated, hidden, arrived = pl.pallas_call(
        functools.partial(kernel, n_t, n_g),
        out_shape=(
            jax.ShapeDtypeStruct((seqs, columns), bf16),
            jax.ShapeDtypeStruct((2, seqs, units), bf16),
            jax.ShapeDtypeStruct((n_t * pairs, span, width), bf16),
        ),
        in_specs=[any_space, vmem, vmem, smem, vmem, vmem, vmem, vmem, any_space, any_space],
        out_specs=(vmem, vmem, any_space),
        scratch_shapes=[
            pltpu.VMEM((pairs, slots, width), bf16),
            pltpu.VMEM((experts, depth, units), bf16),
            pltpu.VMEM((experts, depth, units), bf16),
            pltpu.VMEM((seqs, shares, q_heads, head), bf16),
            pltpu.VMEM((seqs, shares, q_heads, head), f32),
            pltpu.VMEM((seqs, columns), bf16),
            pltpu.VMEM((n_g, seqs, depth + LANES), bf16),
            pltpu.VMEM((n_g, seqs, depth + LANES), bf16),
            pltpu.VMEM((2, 2, n_g * seqs, units), f32),
            pltpu.VMEM((n_g, 2, 2, seqs, units), bf16),
            pltpu.VMEM((n_g, 2, 2, seqs, units), bf16),
            dma,
            dma((experts,)),
            dma((experts,)),
            dma,
            dma((n_t,)),
            dma((n_t,)),
            dma((n_t,)),
            dma((n_t,)),
            dma((n_t,)),
            dma((n_t,)),
            dma((n_g,)),
            dma((n_g,)),
            dma((n_g,)),
            dma((n_g,)),
        ],
        compiler_params=pltpu.CompilerParams(
            collective_id=0, has_side_effects=True, vmem_limit_bytes=60 * 1024 * 1024
        ),
        name="decode_step",
    )(
        key_value_cache,
        queries,
        fresh_key_value,
        lengths,
        residual,
        norm_gain.reshape(1, columns),
        router_weight.T,
        routing.T,
        expert_gate,
        expert_up,
    )
    slot = lax.axis_index("tensor") * span + lax.broadcasted_iota(jnp.int32, (span,), 0)
    new_slot = slot[None, None, :, None] == lengths[:, None, None, None]
    new_cache = jnp.where(
        new_slot,
        fresh_key_value[:, :, None, :],
        arrived.reshape(seqs, kv_heads, span, width),
    )
    return updated, hidden.transpose(1, 0, 2), new_cache


def solution(mesh):
    in_specs = (
        P(("group", "tensor"), None, None),
        P("group", None, None),
        P("group", None, None),
        P("group"),
        P("group", None),
        P(),
        P(),
        P("group", None),
        P(None, "group", "tensor"),
        P(None, "group", "tensor"),
    )
    out_specs = (P("group", None), P("group", None, "tensor"), P("group", None, "tensor", None))
    step = functools.partial(body, mesh.shape["tensor"], mesh.shape["group"])
    return jax.shard_map(step, mesh=mesh, in_specs=in_specs, out_specs=out_specs, check_vma=False)
```

profile of v0, /device:TPU:1, one launch (start us, length us, event | category | flops | bytes accessed | tf_op | source)
XLA Modules:
  0.0 75.3 jit_solution(807891216987875852)
XLA Ops:
  0.6 0.7 broadcast_compare_fusion
  1.4 0.0 copy-start
  1.4 67.3 %decode_step.1 = (bf16[8,6144]{1,0:T(8,128)(2,1)}, bf16[2,8,1024]{2,1,0:T(8,128)(2,1)}, bf16[64,128,256]{2,1,0:T(8,128)(2,1)}) custom-call(bf16[8,1024,256]{2,1,0:T(8,128)(2,1)} %cache_hbm.1, bf16[8,48,128]{2,1,0:T(8,128)(2,1)} %queries_ref.1, bf16[8,8,256]{2,1,0:T(8,128)(2,1)} %fresh_ref.1, s32[8]{0:T(128)} %lengths_ref.1, bf16[8,6144]{1,0:T(8,128)(2,1)} %residual_ref.1, ...), custom_call_target="tpu_custom_call" | custom-call | tf_op jit(solution)/shard_map/decode_step/pallas_call | solution.py:326
  68.6 1.4 %copy.13 = bf16[8,2,1024]{2,1,0:T(2,128)(2,1)} copy(bf16[8,2,1024]{2,0,1:T(8,128)(2,1)} %bitcast.7) | data formatting | bytes 65536
  70.0 0.0 copy-done
  70.0 0.0 copy-start.1
  70.0 4.6 %broadcast_select_fusion = bf16[8,8,128,256]{3,2,1,0:T(8,128)(2,1)} fusion(bf16[8,8,128,256]{3,2,1,0:T(8,128)(2,1)} %bitcast.5, pred[8,128]{1,0:T(8,128)(4,1)S(1)} %broadcast_compare_fusion, bf16[8,8,256]{2,1,0:T(8,128)(2,1)S(1)} %copy-done), kind=kLoop, calls=%fused_computation | loop fusion | flops 2097152 | bytes 8422400 | tf_op jit(solution)/shard_map/jit(_where)/select_n | solution.py:380
  74.7 0.0 copy-done.1
  74.7 0.6 copy.15
  (1 shorter events, 0.0 us)
Async XLA Ops:
  1.4 68.7 %copy-start = (bf16[8,8,256]{2,1,0:T(8,128)(2,1)S(1)}, bf16[8,8,256]{2,1,0:T(8,128)(2,1)}, u32[]{:S(2)}) copy-start(bf16[8,8,256]{2,1,0:T(8,128)(2,1)} %fresh_ref.1) | copy-start | bytes 98308
  70.0 4.6 %copy-start.1 = (bf16[8,6144]{1,0:T(8,128)(2,1)S(1)}, bf16[8,6144]{1,0:T(8,128)(2,1)}, u32[]{:S(2)}) copy-start(bf16[8,6144]{1,0:T(8,128)(2,1)} %get-tuple-element.15) | copy-start | bytes 294916
where the time goes:
time: 75.5 us; the launch traced here: 75.3 us
  Pallas kernels  67.3 us (89%)
  other arithmetic  5.34 us (7%)
  local copies, waits for them, and re-layouts  2.06 us (3%)
    pallas_call x1, Pallas kernels, body(): pl.pallas_call(functools.partial(kernel, n_t, n_g), out_shape=(jax.ShapeD...  67.3 us
    select_n x1, other arithmetic, body(): jnp.where(new_slot, fresh_key_value[:, :, None, :], arrived.reshape(seqs,...  4.6 us
    unnamed x6, local copies, waits for them, and re-layouts  2.06 us

commit v1 on v0

--- a/solution.py
+++ b/solution.py
@@ -32,19 +32,27 @@
     n_t,
     n_g,
     cache_hbm,
+    queries_hbm,
+    fresh_hbm,
+    lengths_hbm,
+    residual_hbm,
+    gain_hbm,
+    router_hbm,
+    routing_hbm,
+    gate_hbm,
+    up_hbm,
+    updated_ref,
+    hidden_ref,
+    arrived,
+    cache_v,
     queries_ref,
     fresh_ref,
+    fresh_rows,
     lengths_ref,
     residual_ref,
     gain_ref,
     router_ref,
     routing_ref,
-    gate_hbm,
-    up_hbm,
-    updated_ref,
-    hidden_ref,
-    out_cache,
-    cache_v,
     gate_v,
     up_v,
     heads_b,
@@ -56,9 +64,9 @@
     p_send,
     p_recv,
     load_sem,
+    small_sem,
     gate_sem,
     up_sem,
-    own_sem,
     a_send_sem,
     a_recv_sem,
     b_send_sem,
@@ -86,13 +94,30 @@
 
     load = pltpu.make_async_copy(cache_hbm, cache_v, load_sem)
     load.start()
-    for e in range(experts):
-        pltpu.make_async_copy(gate_hbm.at[e], gate_v.at[e], gate_sem.at[e]).start()
-        pltpu.make_async_copy(up_hbm.at[e], up_v.at[e], up_sem.at[e]).start()
+    small = [
+        pltpu.make_async_copy(src, dst, small_sem.at[i])
+        for i, (src, dst) in enumerate(
+            (
+                (queries_hbm, queries_ref),
+                (fresh_hbm, fresh_ref),
+                (lengths_hbm, lengths_ref),
+                (routing_hbm, routing_ref),
+                (residual_hbm, residual_ref),
+                (gain_hbm, gain_ref),
+                (router_hbm, router_ref),
+            )
+        )
+    ]
 
     odd = tensor % 2
     t_peers = [
         (1 - odd) * flip(tensor, d, n_t) + odd * flip(tensor, swapped(d, n_t), n_t)
+        for d in range(1, n_t)
+    ]
+    sources = [
+        t_peers[d - 1]
+        if d % 2 == 0
+        else (1 - odd) * flip(tensor, swapped(d, n_t), n_t) + odd * flip(tensor, d, n_t)
         for d in range(1, n_t)
     ]
     g_peers = [flip(group, d, n_g) for d in range(1, n_g)]
@@ -101,6 +126,8 @@
         pl.semaphore_signal(barrier, inc=1, device_id={"tensor": peer}, device_id_type=MESH)
     for peer in g_peers:
         pl.semaphore_signal(barrier, inc=1, device_id={"group": peer}, device_id_type=MESH)
+    for copy in small:
+        copy.start()
     pl.semaphore_wait(barrier, n_t + n_g - 2)
     load.wait()
 
@@ -108,7 +135,7 @@
         peer = t_peers[d - 1]
         return pltpu.make_async_remote_copy(
             src_ref=cache_v.at[pl.ds(begin, count), pl.ds(peer * span, span), :],
-            dst_ref=out_cache.at[pl.ds(tensor * pairs + begin, count)],
+            dst_ref=arrived.at[pl.ds(tensor * pairs + begin, count)],
             send_sem=send.at[d],
             recv_sem=recv.at[d],
             device_id={"tensor": peer},
@@ -118,9 +145,14 @@
     hops = {d: bin(d // 2).count("1") for d in range(1, n_t)}
     order = sorted(range(1, n_t), key=lambda d: (hops[d], d % 2, d))
     near = [d for d in order if hops[d] == 1]
-    early = [block(0, first, d, a_send_sem, a_recv_sem) for d in near]
-    for copy in early:
-        copy.start()
+    early = [(block(0, first, d, a_send_sem, a_recv_sem), d, 0, first) for d in near]
+    for copy, *_ in early:
+        copy.start()
+    for e in range(experts):
+        pltpu.make_async_copy(gate_hbm.at[e], gate_v.at[e], gate_sem.at[e]).start()
+        pltpu.make_async_copy(up_hbm.at[e], up_v.at[e], up_sem.at[e]).start()
+    for copy in small:
+        copy.wait()
 
     begin = tensor * pairs
     seq = begin // kv_heads
@@ -173,16 +205,14 @@
         h_copies.append(copy)
     late = []
     if first < pairs:
-        late = [block(first, pairs - first, d, b_send_sem, b_recv_sem) for d in near]
-    late += [block(0, pairs, d, a_send_sem, a_recv_sem) for d in order if hops[d] != 1]
-    for copy in late:
-        copy.start()
-    own = pltpu.make_async_copy(
-        cache_v.at[:, pl.ds(tensor * span, span), :],
-        out_cache.at[pl.ds(tensor * pairs, pairs)],
-        own_sem,
-    )
-    own.start()
+        rest = pairs - first
+        late = [(block(first, rest, d, b_send_sem, b_recv_sem), d, first, rest) for d in near]
+    late += [
+        (block(0, pairs, d, a_send_sem, a_recv_sem), d, 0, pairs) for d in order if hops[d] != 1
+    ]
+    for copy, *_ in late:
+        copy.start()
+    landings = early + late
     picked[...] = jnp.zeros_like(picked)
     lane = lax.broadcasted_iota(jnp.int32, (seqs, LANES), 1)
     diagonal = lax.broadcasted_iota(jnp.int32, (seqs, seqs), 0) == lax.broadcasted_iota(
@@ -280,6 +310,7 @@
     p_recv[group] = p_send[group]
     for copy in p_copies:
         copy.wait_recv()
+    values = []
     for k in range(2):
         sums = []
         for which in range(2):
@@ -287,14 +318,43 @@
             for g in range(1, n_g):
                 total = total + p_recv[g, k, which].astype(jnp.float32)
             sums.append(total)
-        value = gates[k] * (sums[0] / (1.0 + jnp.exp(-sums[0]))) * sums[1]
-        hidden_ref[k] = value.astype(jnp.bfloat16)
-
+        values.append(gates[k] * (sums[0] / (1.0 + jnp.exp(-sums[0]))) * sums[1])
+    hidden_ref[...] = jnp.stack(values, axis=1).astype(jnp.bfloat16)
+
+    fresh_rows[...] = fresh_ref[...].astype(jnp.float32).reshape(fresh_rows.shape)
+    slot = lax.broadcasted_iota(jnp.int32, (span, width), 0).astype(jnp.float32).astype(jnp.bfloat16)
+
+    def patch(source, begin, count):
+        row = source * pairs + begin
+        owner = row // kv_heads
+        local = (lengths_ref[owner] - tensor * span).astype(jnp.float32).astype(jnp.bfloat16)
+        here = slot == local
+        for p in range(count):
+            new = fresh_rows[pl.ds(row + p, 1), :].astype(jnp.bfloat16)
+            yield p, row + p, here, new
+
+    for p, at, here, new in patch(tensor, 0, pairs):
+        arrived[at] = jnp.where(here, new, cache_v[p, pl.ds(tensor * span, span), :])
     for copy in h_copies + x_copies + p_copies:
         copy.wait_send()
-    for copy in early + late:
+    for copy, d, begin, count in landings:
+        copy.wait_recv()
+        for p, at, here, new in patch(sources[d - 1], begin, count):
+            arrived[at] = jnp.where(here, new, arrived[at])
+    for copy, d, begin, count in landings:
+        copy.wait_send()
+
+
+def finish(updated, hidden, arrived, updated_out, hidden_out, cache_out, sem):
+    copies = [
+        pltpu.make_async_copy(arrived, cache_out, sem.at[0]),
+        pltpu.make_async_copy(updated, updated_out, sem.at[1]),
+        pltpu.make_async_copy(hidden, hidden_out, sem.at[2]),
+    ]
+    for copy in copies:
+        copy.start()
+    for copy in copies:
         copy.wait()
-    own.wait()
 
 
 def body(
@@ -318,22 +378,30 @@
     experts, depth, units = expert_gate.shape
     span = slots // n_t
     shares = kv_heads // pairs
-    any_space = pl.BlockSpec(memory_space=pl.ANY)
+    bf16, f32 = jnp.bfloat16, jnp.float32
+    hbm = pl.BlockSpec(memory_space=pltpu.HBM)
     vmem = pl.BlockSpec(memory_space=pltpu.VMEM)
-    smem = pl.BlockSpec(memory_space=pltpu.SMEM)
     dma = pltpu.SemaphoreType.DMA
-    bf16, f32 = jnp.bfloat16, jnp.float32
+    rows = n_t * pairs
     updated, hidden, arrived = pl.pallas_call(
         functools.partial(kernel, n_t, n_g),
         out_shape=(
-            jax.ShapeDtypeStruct((seqs, columns), bf16),
-            jax.ShapeDtypeStruct((2, seqs, units), bf16),
-            jax.ShapeDtypeStruct((n_t * pairs, span, width), bf16),
+            pltpu.VMEM((seqs, columns), bf16),
+            pltpu.VMEM((seqs, 2, units), bf16),
+            pltpu.VMEM((rows, span, width), bf16),
         ),
-        in_specs=[any_space, vmem, vmem, smem, vmem, vmem, vmem, vmem, any_space, any_space],
-        out_specs=(vmem, vmem, any_space),
+        in_specs=[hbm] * 10,
+        out_specs=(vmem, vmem, vmem),
         scratch_shapes=[
             pltpu.VMEM((pairs, slots, width), bf16),
+            pltpu.VMEM(queries.shape, bf16),
+            pltpu.VMEM(fresh_key_value.shape, bf16),
+            pltpu.VMEM((rows, width), f32),
+            pltpu.SMEM(lengths.shape, jnp.int32),
+            pltpu.VMEM(residual.shape, bf16),
+            pltpu.VMEM((1, columns), f32),
+            pltpu.VMEM((experts, columns), bf16),
+            pltpu.VMEM((2, seqs), jnp.int32),
             pltpu.VMEM((experts, depth, units), bf16),
             pltpu.VMEM((experts, depth, units), bf16),
             pltpu.VMEM((seqs, shares, q_heads, head), bf16),
@@ -345,9 +413,9 @@
             pltpu.VMEM((n_g, 2, 2, seqs, units), bf16),
             pltpu.VMEM((n_g, 2, 2, seqs, units), bf16),
             dma,
+            dma((7,)),
             dma((experts,)),
             dma((experts,)),
-            dma,
             dma((n_t,)),
             dma((n_t,)),
             dma((n_t,)),
@@ -360,7 +428,7 @@
             dma((n_g,)),
         ],
         compiler_params=pltpu.CompilerParams(
-            collective_id=0, has_side_effects=True, vmem_limit_bytes=60 * 1024 * 1024
+            collective_id=0, has_side_effects=True, vmem_limit_bytes=57 * 1024 * 1024
         ),
         name="decode_step",
     )(
@@ -375,14 +443,20 @@
         expert_gate,
         expert_up,
     )
-    slot = lax.axis_index("tensor") * span + lax.broadcasted_iota(jnp.int32, (span,), 0)
-    new_slot = slot[None, None, :, None] == lengths[:, None, None, None]
-    new_cache = jnp.where(
-        new_slot,
-        fresh_key_value[:, :, None, :],
-        arrived.reshape(seqs, kv_heads, span, width),
-    )
-    return updated, hidden.transpose(1, 0, 2), new_cache
+    updated, hidden, new_cache = pl.pallas_call(
+        finish,
+        out_shape=(
+            jax.ShapeDtypeStruct(updated.shape, bf16),
+            jax.ShapeDtypeStruct(hidden.shape, bf16),
+            jax.ShapeDtypeStruct(arrived.shape, bf16),
+        ),
+        in_specs=[vmem] * 3,
+        out_specs=[hbm] * 3,
+        scratch_shapes=[dma((3,))],
+        compiler_params=pltpu.CompilerParams(vmem_limit_bytes=1024 * 1024),
+        name="hand_over",
+    )(*(pltpu.with_memory_space_constraint(x, pltpu.VMEM) for x in (updated, hidden, arrived)))
+    return updated, hidden, new_cache.reshape(seqs, kv_heads, span, width)
 
 
 def solution(mesh):

time: 75.5 us -> 57 us (0.75)
  Pallas kernels: 67.3 us -> 56.3 us
  other arithmetic: 5.34 us -> 0 us
  local copies, waits for them, and re-layouts: 2.06 us -> 0 us
    pallas_call x1 -> x2, Pallas kernels: 67.3 us -> 56.3 us  [the longest x1 54.2 us: body(): pl.pallas_call(functools.partial(kernel, n_t, n_g), out_shape=(pltpu.VMEM...]
    select_n x1 -> x0, other arithmetic: 4.6 us -> none  [body(): jnp.where(new_slot, fresh_key_value[:, :, None, :], arrived.reshape(seqs,...]
    unnamed x6 -> x0, local copies, waits for them, and re-layouts: 2.06 us -> none
where the time goes in v1:
time: 57 us; the launch traced here: 56.9 us
  Pallas kernels  56.3 us (99%)
  between operations  0.64 us (1%)
    pallas_call x1, Pallas kernels, body(): pl.pallas_call(functools.partial(kernel, n_t, n_g), out_shape=(pltpu.VMEM...  54.2 us
    pallas_call x1, Pallas kernels, body(): pl.pallas_call(finish, out_shape=(jax.ShapeDtypeStruct(updated.shape, bf1...  2.05 us

profile of v1, /device:TPU:1, one launch (start us, length us, event | category | flops | bytes accessed | tf_op | source)
XLA Modules:
  0.0 56.9 jit_solution(9887852177785218769)
XLA Ops:
  0.6 54.2 %decode_step.1 = (bf16[8,6144]{1,0:T(8,128)(2,1)S(1)}, bf16[8,2,1024]{2,1,0:T(2,128)(2,1)S(1)}, bf16[64,128,256]{2,1,0:T(8,128)(2,1)S(1)}) custom-call(bf16[8,1024,256]{2,1,0:T(8,128)(2,1)} %cache_hbm.1, bf16[8,48,128]{2,1,0:T(8,128)(2,1)} %queries_hbm.1, bf16[8,8,256]{2,1,0:T(8,128)(2,1)} %fresh_hbm.1, s32[8]{0:T(128)} %lengths_hbm.1, ...), custom_call_target="tpu_custom_call" | custom-call | tf_op jit(solution)/shard_map/decode_step/pallas_call | solution.py:386
  54.8 2.1 %hand_over.1 = (bf16[8,6144]{1,0:T(8,128)(2,1)}, bf16[8,2,1024]{2,1,0:T(2,128)(2,1)}, bf16[64,128,256]{2,1,0:T(8,128)(2,1)}) custom-call(bf16[8,6144]{1,0:T(8,128)(2,1)S(1)} %get-tuple-element.9.updated, bf16[8,2,1024]{2,1,0:T(2,128)(2,1)S(1)} %get-tuple-element.10.hidden, bf16[64,128,256]{2,1,0:T(8,128)(2,1)S(1)} %get-tuple-element.11.arrived), custom_call_target="tpu_custom_call" | custom-call | tf_op jit(solution)/shard_map/hand_over/pallas_call | solution.py:446

commit v2 on v1

--- a/solution.py
+++ b/solution.py
@@ -26,6 +26,77 @@
     if count < 8 or (bits >> 1) % 2 == (bits >> 2) % 2:
         return bits
     return bits ^ 6
+
+
+class enter:
+    def __init__(self, n_t, n_g, tensor, group, t_peers, g_peers, go_sem, far_sem, z_sem):
+        self.barrier = pltpu.get_barrier_semaphore()
+        self.relayed = n_t == 8
+        self.tensor, self.n_t, self.n_g = tensor, n_t, n_g
+        self.t_peers, self.g_peers = t_peers, g_peers
+        self.sems = go_sem, far_sem, z_sem
+        self.lead = tensor % 2 == 1
+        if not self.relayed:
+            for peer in t_peers:
+                self.signal(self.barrier, {"tensor": peer})
+            for peer in g_peers:
+                self.signal(self.barrier, {"group": peer})
+            return
+        base = tensor - tensor % 2 + 1
+        for bits in (2, 4):
+            self.signal(self.barrier, {"tensor": flip(base, bits, n_t)})
+
+        @pl.when(jnp.logical_not(self.lead))
+        def _():
+            self.signal(self.barrier, {"tensor": base})
+
+    def signal(self, sem, peer):
+        pl.semaphore_signal(sem, inc=1, device_id=peer, device_id_type=MESH)
+
+    def near(self):
+        if not self.relayed:
+            pl.semaphore_wait(self.barrier, self.n_t + self.n_g - 2)
+            return
+        go_sem, far_sem, _ = self.sems
+        mate = flip(self.tensor, 1, self.n_t)
+
+        @pl.when(self.lead)
+        def _():
+            pl.semaphore_wait(self.barrier, 5)
+            self.signal(go_sem, {"tensor": mate})
+            for bits in (2, 3):
+                self.signal(far_sem, {"tensor": flip(self.tensor, bits, self.n_t)})
+
+        @pl.when(jnp.logical_not(self.lead))
+        def _():
+            pl.semaphore_wait(go_sem, 1)
+
+    def relay(self):
+        if self.relayed:
+
+            @pl.when(jnp.logical_not(self.lead))
+            def _():
+                for peer in self.g_peers:
+                    self.signal(self.barrier, {"group": peer})
+
+    def distant(self):
+        if self.relayed:
+            pl.semaphore_wait(self.sems[1], 1)
+
+    def groups(self):
+        if not self.relayed:
+            return
+        z_sem = self.sems[2]
+        mate = flip(self.tensor, 1, self.n_t)
+
+        @pl.when(jnp.logical_not(self.lead))
+        def _():
+            pl.semaphore_wait(self.barrier, self.n_g - 1)
+            self.signal(z_sem, {"tensor": mate})
+
+        @pl.when(self.lead)
+        def _():
+            pl.semaphore_wait(z_sem, 1)
 
 
 def kernel(
@@ -71,36 +142,55 @@
     a_recv_sem,
     b_send_sem,
     b_recv_sem,
+    c_send_sem,
+    c_recv_sem,
     h_send_sem,
     h_recv_sem,
     x_send_sem,
     x_recv_sem,
     p_send_sem,
     p_recv_sem,
+    go_sem,
+    far_sem,
+    z_sem,
 ):
     tensor = lax.axis_index("tensor")
     group = lax.axis_index("group")
     pairs, slots, width = cache_v.shape
     head = width // 2
     span = slots // n_t
-    first = max(1, pairs // 2)
-    seqs, q_heads, _ = queries_ref.shape
-    kv_heads = fresh_ref.shape[1]
+    cut = max(1, 3 * pairs // 8)
+    later = max(cut, 5 * pairs // 8)
+    seqs = residual_ref.shape[0]
+    q_heads = queries_ref.shape[0]
+    kv_heads = fresh_ref.shape[0]
     per = q_heads // kv_heads
     experts = gate_v.shape[0]
     depth = gate_v.shape[1]
     columns = residual_ref.shape[1]
     shares = heads_v.shape[1]
 
-    load = pltpu.make_async_copy(cache_hbm, cache_v, load_sem)
-    load.start()
+    begin = tensor * pairs
+    seq = begin // kv_heads
+    head0 = begin % kv_heads
+    share = tensor % shares
+    odd = tensor % 2
+    t_peers = [
+        (1 - odd) * flip(tensor, d, n_t) + odd * flip(tensor, swapped(d, n_t), n_t)
+        for d in range(1, n_t)
+    ]
+    g_peers = [flip(group, d, n_g) for d in range(1, n_g)]
+    hops = {d: bin(d // 2).count("1") for d in range(1, n_t)}
+    order = sorted(range(1, n_t), key=lambda d: (hops[d], d % 2, d))
+    near = [d for d in order if hops[d] == 1]
+    far = [d for d in order if hops[d] > 1]
     small = [
         pltpu.make_async_copy(src, dst, small_sem.at[i])
         for i, (src, dst) in enumerate(
             (
-                (queries_hbm, queries_ref),
-                (fresh_hbm, fresh_ref),
                 (lengths_hbm, lengths_ref),
+                (fresh_hbm.at[seq], fresh_ref),
+                (queries_hbm.at[seq], queries_ref),
                 (routing_hbm, routing_ref),
                 (residual_hbm, residual_ref),
                 (gain_hbm, gain_ref),
@@ -109,59 +199,72 @@
         )
     ]
 
-    odd = tensor % 2
-    t_peers = [
-        (1 - odd) * flip(tensor, d, n_t) + odd * flip(tensor, swapped(d, n_t), n_t)
-        for d in range(1, n_t)
-    ]
-    sources = [
-        t_peers[d - 1]
-        if d % 2 == 0
-        else (1 - odd) * flip(tensor, swapped(d, n_t), n_t) + odd * flip(tensor, d, n_t)
-        for d in range(1, n_t)
-    ]
-    g_peers = [flip(group, d, n_g) for d in range(1, n_g)]
-    barrier = pltpu.get_barrier_semaphore()
-    for peer in t_peers:
-        pl.semaphore_signal(barrier, inc=1, device_id={"tensor": peer}, device_id_type=MESH)
-    for peer in g_peers:
-        pl.semaphore_signal(barrier, inc=1, device_id={"group": peer}, device_id_type=MESH)
-    for copy in small:
-        copy.start()
-    pl.semaphore_wait(barrier, n_t + n_g - 2)
-    load.wait()
-
-    def block(begin, count, d, send, recv):
+    def slab(peer):
+        return pl.ds(pl.multiple_of(peer * span, span), span)
+
+    def fetch(d, first_row, count):
+        peer = tensor if d == 0 else t_peers[d - 1]
+        rows = pl.ds(first_row, count), slab(peer)
+        at = d if first_row == 0 else n_t + d
+        return pltpu.make_async_copy(cache_hbm.at[rows], cache_v.at[rows], load_sem.at[at])
+
+    greet = enter(n_t, n_g, tensor, group, t_peers, g_peers, go_sem, far_sem, z_sem)
+    loads = [fetch(d, 0, cut) for d in near]
+    more = [fetch(d, cut, pairs - cut) for d in near if cut < pairs]
+    more += [fetch(d, 0, pairs) for d in far + [1, 0]]
+    small[0].start()
+    small[1].start()
+    for copy in loads + more:
+        copy.start()
+    for copy in small[2:]:
+        copy.start()
+
+    def block(first_row, count, d, send, recv):
         peer = t_peers[d - 1]
         return pltpu.make_async_remote_copy(
-            src_ref=cache_v.at[pl.ds(begin, count), pl.ds(peer * span, span), :],
-            dst_ref=arrived.at[pl.ds(tensor * pairs + begin, count)],
+            src_ref=cache_v.at[pl.ds(first_row, count), slab(peer), :],
+            dst_ref=arrived.at[pl.ds(begin + first_row, count)],
             send_sem=send.at[d],
             recv_sem=recv.at[d],
             device_id={"tensor": peer},
             device_id_type=MESH,
         )
 
-    hops = {d: bin(d // 2).count("1") for d in range(1, n_t)}
-    order = sorted(range(1, n_t), key=lambda d: (hops[d], d % 2, d))
-    near = [d for d in order if hops[d] == 1]
-    early = [(block(0, first, d, a_send_sem, a_recv_sem), d, 0, first) for d in near]
-    for copy, *_ in early:
-        copy.start()
+    slot = lax.broadcasted_iota(jnp.int32, (span, width), 0).astype(jnp.float32)
+    slot = slot.astype(jnp.bfloat16)
+    small[0].wait()
+    small[1].wait()
+    length = lengths_ref[seq]
+    fresh_rows[...] = fresh_ref[...].astype(jnp.float32)
+
+    def patched(peer, p):
+        here = slot == (length - peer * span).astype(jnp.float32).astype(jnp.bfloat16)
+        new = fresh_rows[pl.ds(head0 + p, 1), :].astype(jnp.bfloat16)
+        return jnp.where(here, new, cache_v[p, slab(peer), :])
+
+    def patch(peer, first_row, count):
+        for p in range(first_row, first_row + count):
+            cache_v[p, slab(peer), :] = patched(peer, p)
+
+    for d, copy in zip(near, loads):
+        copy.wait()
+        patch(t_peers[d - 1], 0, cut)
+    greet.near()
+    early = [block(0, cut, d, a_send_sem, a_recv_sem) for d in near]
+    for copy in early:
+        copy.start()
+    greet.relay()
     for e in range(experts):
         pltpu.make_async_copy(gate_hbm.at[e], gate_v.at[e], gate_sem.at[e]).start()
         pltpu.make_async_copy(up_hbm.at[e], up_v.at[e], up_sem.at[e]).start()
-    for copy in small:
+    for copy in more:
         copy.wait()
-
-    begin = tensor * pairs
-    seq = begin // kv_heads
-    head0 = begin % kv_heads
-    share = tensor % shares
+    for copy in small[2:]:
+        copy.wait()
+
     scale = 1.0 / math.sqrt(head)
-    q = queries_ref[seq]
-    fresh = fresh_ref[seq]
-    length = lengths_ref[seq]
+    q = queries_ref[...]
+    fresh = fresh_ref[...]
     row = lax.broadcasted_iota(jnp.int32, (q_heads, 1), 0)
     mine = [
         (row >= (head0 + p) * per) & (row < (head0 + p + 1) * per) for p in range(pairs)
@@ -191,28 +294,37 @@
         result = jnp.where(mine[p], (o + own_value) / denominator, result)
     heads_b[seq, share] = result.astype(jnp.bfloat16)
 
-    h_copies = []
-    for d in order:
-        copy = pltpu.make_async_remote_copy(
-            src_ref=heads_b.at[seq, share],
-            dst_ref=heads_b.at[seq, share],
+    def pass_heads(owner, d, peer):
+        at = owner * pairs // kv_heads, owner % shares
+        return pltpu.make_async_remote_copy(
+            src_ref=heads_b.at[at],
+            dst_ref=heads_b.at[at],
             send_sem=h_send_sem.at[d],
             recv_sem=h_recv_sem.at[d],
-            device_id={"tensor": t_peers[d - 1]},
+            device_id={"tensor": peer},
             device_id_type=MESH,
         )
-        copy.start()
-        h_copies.append(copy)
-    late = []
-    if first < pairs:
-        rest = pairs - first
-        late = [(block(first, rest, d, b_send_sem, b_recv_sem), d, first, rest) for d in near]
-    late += [
-        (block(0, pairs, d, a_send_sem, a_recv_sem), d, 0, pairs) for d in order if hops[d] != 1
-    ]
-    for copy, *_ in late:
-        copy.start()
-    landings = early + late
+
+    greet.distant()
+    mate = t_peers[0]
+    same = [d for d in order if d % 2 == 0]
+    h_copies = {d: pass_heads(tensor, d, t_peers[d - 1]) for d in same + [1]}
+    for copy in h_copies.values():
+        copy.start()
+    for d in near:
+        patch(t_peers[d - 1], cut, later - cut)
+    patch(mate, 0, pairs)
+    middle = [block(0, pairs, 1, a_send_sem, a_recv_sem)]
+    if cut < later:
+        middle += [block(cut, later - cut, d, c_send_sem, c_recv_sem) for d in near]
+    for copy in middle:
+        copy.start()
+    for d in far:
+        patch(t_peers[d - 1], 0, pairs)
+    for d in near:
+        patch(t_peers[d - 1], later, pairs - later)
+    for p in range(pairs):
+        arrived[begin + p] = patched(tensor, p)
     picked[...] = jnp.zeros_like(picked)
     lane = lax.broadcasted_iota(jnp.int32, (seqs, LANES), 1)
     diagonal = lax.broadcasted_iota(jnp.int32, (seqs, seqs), 0) == lax.broadcasted_iota(
@@ -229,8 +341,18 @@
     tags = jnp.where(lane == 0, ids[0], jnp.where(lane == 1, ids[1], 0.0)).astype(jnp.bfloat16)
     for g in range(n_g):
         x_send[g, :, depth:] = tags
-    for copy in h_copies:
-        copy.wait_recv()
+    for d in same:
+        h_copies[d].wait_recv()
+        h_copies[d + 1] = pass_heads(t_peers[d - 1], d + 1, mate)
+        h_copies[d + 1].start()
+    late = [block(0, pairs, d, a_send_sem, a_recv_sem) for d in far]
+    if later < pairs:
+        late += [block(later, pairs - later, d, b_send_sem, b_recv_sem) for d in near]
+    for copy in late:
+        copy.start()
+    h_copies[1].wait_recv()
+    for d in same:
+        h_copies[d + 1].wait_recv()
 
     heads_v[...] = heads_b[...].astype(jnp.float32)
 
@@ -249,6 +371,7 @@
         n = (u * factor * gain_ref[:, c : c + LANES]).astype(jnp.bfloat16)
         normed_v[:, c : c + LANES] = n
         x_send[c // depth, :, c % depth : c % depth + LANES] = n
+    greet.groups()
     x_copies = []
     for d in range(1, n_g):
         copy = pltpu.make_async_remote_copy(
@@ -321,36 +444,22 @@
         values.append(gates[k] * (sums[0] / (1.0 + jnp.exp(-sums[0]))) * sums[1])
     hidden_ref[...] = jnp.stack(values, axis=1).astype(jnp.bfloat16)
 
-    fresh_rows[...] = fresh_ref[...].astype(jnp.float32).reshape(fresh_rows.shape)
-    slot = lax.broadcasted_iota(jnp.int32, (span, width), 0).astype(jnp.float32).astype(jnp.bfloat16)
-
-    def patch(source, begin, count):
-        row = source * pairs + begin
-        owner = row // kv_heads
-        local = (lengths_ref[owner] - tensor * span).astype(jnp.float32).astype(jnp.bfloat16)
-        here = slot == local
-        for p in range(count):
-            new = fresh_rows[pl.ds(row + p, 1), :].astype(jnp.bfloat16)
-            yield p, row + p, here, new
-
-    for p, at, here, new in patch(tensor, 0, pairs):
-        arrived[at] = jnp.where(here, new, cache_v[p, pl.ds(tensor * span, span), :])
-    for copy in h_copies + x_copies + p_copies:
+    for copy in list(h_copies.values()) + x_copies + p_copies:
         copy.wait_send()
-    for copy, d, begin, count in landings:
-        copy.wait_recv()
-        for p, at, here, new in patch(sources[d - 1], begin, count):
-            arrived[at] = jnp.where(here, new, arrived[at])
-    for copy, d, begin, count in landings:
-        copy.wait_send()
-
-
-def finish(updated, hidden, arrived, updated_out, hidden_out, cache_out, sem):
+    for copy in early + middle + late:
+        copy.wait()
+
+
+def finish(pieces, updated, hidden, arrived, updated_out, hidden_out, cache_out, sem):
+    count = arrived.shape[0] // pieces
     copies = [
-        pltpu.make_async_copy(arrived, cache_out, sem.at[0]),
-        pltpu.make_async_copy(updated, updated_out, sem.at[1]),
-        pltpu.make_async_copy(hidden, hidden_out, sem.at[2]),
+        pltpu.make_async_copy(
+            arrived.at[pl.ds(i * count, count)], cache_out.at[pl.ds(i * count, count)], sem.at[i]
+        )
+        for i in range(pieces)
     ]
+    copies.append(pltpu.make_async_copy(updated, updated_out, sem.at[pieces]))
+    copies.append(pltpu.make_async_copy(hidden, hidden_out, sem.at[pieces + 1]))
     for copy in copies:
         copy.start()
     for copy in copies:
@@ -382,6 +491,7 @@
     hbm = pl.BlockSpec(memory_space=pltpu.HBM)
     vmem = pl.BlockSpec(memory_space=pltpu.VMEM)
     dma = pltpu.SemaphoreType.DMA
+    regular = pltpu.SemaphoreType.REGULAR
     rows = n_t * pairs
     updated, hidden, arrived = pl.pallas_call(
         functools.partial(kernel, n_t, n_g),
@@ -394,9 +504,9 @@
         out_specs=(vmem, vmem, vmem),
         scratch_shapes=[
             pltpu.VMEM((pairs, slots, width), bf16),
-            pltpu.VMEM(queries.shape, bf16),
-            pltpu.VMEM(fresh_key_value.shape, bf16),
-            pltpu.VMEM((rows, width), f32),
+            pltpu.VMEM((q_heads, head), bf16),
+            pltpu.VMEM((kv_heads, width), bf16),
+            pltpu.VMEM((kv_heads, width), f32),
             pltpu.SMEM(lengths.shape, jnp.int32),
             pltpu.VMEM(residual.shape, bf16),
             pltpu.VMEM((1, columns), f32),
@@ -412,10 +522,12 @@
             pltpu.VMEM((2, 2, n_g * seqs, units), f32),
             pltpu.VMEM((n_g, 2, 2, seqs, units), bf16),
             pltpu.VMEM((n_g, 2, 2, seqs, units), bf16),
-            dma,
+            dma((2 * n_t,)),
             dma((7,)),
             dma((experts,)),
             dma((experts,)),
+            dma((n_t,)),
+            dma((n_t,)),
             dma((n_t,)),
             dma((n_t,)),
             dma((n_t,)),
@@ -426,6 +538,9 @@
             dma((n_g,)),
             dma((n_g,)),
             dma((n_g,)),
+            regular,
+            regular,
+            regular,
         ],
         compiler_params=pltpu.CompilerParams(
             collective_id=0, has_side_effects=True, vmem_limit_bytes=57 * 1024 * 1024
@@ -444,7 +559,7 @@
         expert_up,
     )
     updated, hidden, new_cache = pl.pallas_call(
-        finish,
+        functools.partial(finish, 8),
         out_shape=(
             jax.ShapeDtypeStruct(updated.shape, bf16),
             jax.ShapeDtypeStruct(hidden.shape, bf16),
@@ -452,7 +567,7 @@
         ),
         in_specs=[vmem] * 3,
         out_specs=[hbm] * 3,
-        scratch_shapes=[dma((3,))],
+        scratch_shapes=[dma((10,))],
         compiler_params=pltpu.CompilerParams(vmem_limit_bytes=1024 * 1024),
         name="hand_over",
     )(*(pltpu.with_memory_space_constraint(x, pltpu.VMEM) for x in (updated, hidden, arrived)))

time: 57 us -> 54.4 us (0.954)
  Pallas kernels: 56.3 us -> 53.6 us
    pallas_call x1, Pallas kernels: 54.2 us -> 51.5 us  [body(): pl.pallas_call(functools.partial(kernel, n_t, n_g), out_shape=(pltpu.VMEM...]
where the time goes in v2:
time: 54.4 us; the launch traced here: 54.2 us
  Pallas kernels  53.6 us (99%)
  between operations  0.64 us (1%)
    pallas_call x1, Pallas kernels, body(): pl.pallas_call(functools.partial(kernel, n_t, n_g), out_shape=(pltpu.VMEM...  51.5 us
    pallas_call x1, Pallas kernels, body(): pl.pallas_call(functools.partial(finish, 8), out_shape=(jax.ShapeDtypeStr...  2.11 us

profile of v2, /device:TPU:1, one launch (start us, length us, event | category | flops | bytes accessed | tf_op | source)
XLA Modules:
  0.0 54.2 jit_solution(17745542732556951019)
XLA Ops:
  0.6 51.5 %decode_step.1 = (bf16[8,6144]{1,0:T(8,128)(2,1)S(1)}, bf16[8,2,1024]{2,1,0:T(2,128)(2,1)S(1)}, bf16[64,128,256]{2,1,0:T(8,128)(2,1)S(1)}) custom-call(bf16[8,1024,256]{2,1,0:T(8,128)(2,1)} %cache_hbm.1, bf16[8,48,128]{2,1,0:T(8,128)(2,1)} %queries_hbm.1, bf16[8,8,256]{2,1,0:T(8,128)(2,1)} %fresh_hbm.1, s32[8]{0:T(128)} %lengths_hbm.1, ...), custom_call_target="tpu_custom_call" | custom-call | tf_op jit(solution)/shard_map/decode_step/pallas_call | solution.py:496
  52.1 2.1 %hand_over.1 = (bf16[8,6144]{1,0:T(8,128)(2,1)}, bf16[8,2,1024]{2,1,0:T(2,128)(2,1)}, bf16[64,128,256]{2,1,0:T(8,128)(2,1)}) custom-call(bf16[8,6144]{1,0:T(8,128)(2,1)S(1)} %get-tuple-element.9.updated, bf16[8,2,1024]{2,1,0:T(2,128)(2,1)S(1)} %get-tuple-element.10.hidden, bf16[64,128,256]{2,1,0:T(8,128)(2,1)S(1)} %get-tuple-element.11.arrived), custom_call_target="tpu_custom_call" | custom-call | tf_op jit(solution)/shard_map/hand_over/pallas_call | solution.py:561

commit v3 on v2

--- a/solution.py
+++ b/solution.py
@@ -29,12 +29,12 @@
 
 
 class enter:
-    def __init__(self, n_t, n_g, tensor, group, t_peers, g_peers, go_sem, far_sem, z_sem):
+    def __init__(self, n_t, n_g, tensor, t_peers, g_peers, *sems):
         self.barrier = pltpu.get_barrier_semaphore()
         self.relayed = n_t == 8
         self.tensor, self.n_t, self.n_g = tensor, n_t, n_g
         self.t_peers, self.g_peers = t_peers, g_peers
-        self.sems = go_sem, far_sem, z_sem
+        self.sems = sems
         self.lead = tensor % 2 == 1
         if not self.relayed:
             for peer in t_peers:
@@ -43,8 +43,11 @@
                 self.signal(self.barrier, {"group": peer})
             return
         base = tensor - tensor % 2 + 1
-        for bits in (2, 4):
-            self.signal(self.barrier, {"tensor": flip(base, bits, n_t)})
+
+        @pl.when(self.lead)
+        def _():
+            for bits in (2, 4):
+                self.signal(self.barrier, {"tensor": flip(tensor, bits, n_t)})
 
         @pl.when(jnp.logical_not(self.lead))
         def _():
@@ -57,19 +60,30 @@
         if not self.relayed:
             pl.semaphore_wait(self.barrier, self.n_t + self.n_g - 2)
             return
-        go_sem, far_sem, _ = self.sems
-        mate = flip(self.tensor, 1, self.n_t)
+        go_sem, pair_sem = self.sems[0], self.sems[3]
 
         @pl.when(self.lead)
         def _():
-            pl.semaphore_wait(self.barrier, 5)
+            pl.semaphore_wait(self.barrier, 3)
+            for bits in (2, 4):
+                self.signal(pair_sem, {"tensor": flip(self.tensor, bits, self.n_t)})
+
+        @pl.when(jnp.logical_not(self.lead))
+        def _():
+            pl.semaphore_wait(go_sem, 1)
+
+    def cross(self):
+        if not self.relayed:
+            return
+        go_sem, far_sem, _, pair_sem = self.sems
+        mate = flip(self.tensor, 1, self.n_t)
+
+        @pl.when(self.lead)
+        def _():
+            pl.semaphore_wait(pair_sem, 2)
             self.signal(go_sem, {"tensor": mate})
             for bits in (2, 3):
                 self.signal(far_sem, {"tensor": flip(self.tensor, bits, self.n_t)})
-
-        @pl.when(jnp.logical_not(self.lead))
-        def _():
-            pl.semaphore_wait(go_sem, 1)
 
     def relay(self):
         if self.relayed:
@@ -153,6 +167,7 @@
     go_sem,
     far_sem,
     z_sem,
+    pair_sem,
 ):
     tensor = lax.axis_index("tensor")
     group = lax.axis_index("group")
@@ -208,7 +223,7 @@
         at = d if first_row == 0 else n_t + d
         return pltpu.make_async_copy(cache_hbm.at[rows], cache_v.at[rows], load_sem.at[at])
 
-    greet = enter(n_t, n_g, tensor, group, t_peers, g_peers, go_sem, far_sem, z_sem)
+    greet = enter(n_t, n_g, tensor, t_peers, g_peers, go_sem, far_sem, z_sem, pair_sem)
     loads = [fetch(d, 0, cut) for d in near]
     more = [fetch(d, cut, pairs - cut) for d in near if cut < pairs]
     more += [fetch(d, 0, pairs) for d in far + [1, 0]]
@@ -251,7 +266,11 @@
         patch(t_peers[d - 1], 0, cut)
     greet.near()
     early = [block(0, cut, d, a_send_sem, a_recv_sem) for d in near]
-    for copy in early:
+    straight = sum(d % 2 == 0 for d in near)
+    for copy in early[:straight]:
+        copy.start()
+    greet.cross()
+    for copy in early[straight:]:
         copy.start()
     greet.relay()
     for e in range(experts):
@@ -541,6 +560,7 @@
             regular,
             regular,
             regular,
+            regular,
         ],
         compiler_params=pltpu.CompilerParams(
             collective_id=0, has_side_effects=True, vmem_limit_bytes=57 * 1024 * 1024

time: 54.4 us -> 54 us (level)
  no operation moved by 1% of the time
where the time goes in v3:
time: 54 us; the launch traced here: 53.8 us
  Pallas kernels  53.2 us (99%)
  between operations  0.64 us (1%)
    pallas_call x1, Pallas kernels, body(): pl.pallas_call(functools.partial(kernel, n_t, n_g), out_shape=(pltpu.VMEM...  51.1 us
    pallas_call x1, Pallas kernels, body(): pl.pallas_call(functools.partial(finish, 8), out_shape=(jax.ShapeDtypeStr...  2.11 us

profile of v3, /device:TPU:1, one launch (start us, length us, event | category | flops | bytes accessed | tf_op | source)
XLA Modules:
  0.0 53.8 jit_solution(4719584373791921964)
XLA Ops:
  0.6 51.1 %decode_step.1 = (bf16[8,6144]{1,0:T(8,128)(2,1)S(1)}, bf16[8,2,1024]{2,1,0:T(2,128)(2,1)S(1)}, bf16[64,128,256]{2,1,0:T(8,128)(2,1)S(1)}) custom-call(bf16[8,1024,256]{2,1,0:T(8,128)(2,1)} %cache_hbm.1, bf16[8,48,128]{2,1,0:T(8,128)(2,1)} %queries_hbm.1, bf16[8,8,256]{2,1,0:T(8,128)(2,1)} %fresh_hbm.1, s32[8]{0:T(128)} %lengths_hbm.1, ...), custom_call_target="tpu_custom_call" | custom-call | tf_op jit(solution)/shard_map/decode_step/pallas_call | solution.py:515
  51.7 2.1 %hand_over.1 = (bf16[8,6144]{1,0:T(8,128)(2,1)}, bf16[8,2,1024]{2,1,0:T(2,128)(2,1)}, bf16[64,128,256]{2,1,0:T(8,128)(2,1)}) custom-call(bf16[8,6144]{1,0:T(8,128)(2,1)S(1)} %get-tuple-element.9.updated, bf16[8,2,1024]{2,1,0:T(2,128)(2,1)S(1)} %get-tuple-element.10.hidden, bf16[64,128,256]{2,1,0:T(8,128)(2,1)S(1)} %get-tuple-element.11.arrived), custom_call_target="tpu_custom_call" | custom-call | tf_op jit(solution)/shard_map/hand_over/pallas_call | solution.py:581
